TPU v7x, 32 devices: a whole 2x2x4 slice. The times are simulated.
32 devices in a mesh: patch: 2 (over core), theta: 4 (over z), phi: 4 (over y, x).
Axes of the slice: x: 2, y: 2, z: 4, core: 2. Of those that a mesh axis runs over, the one named last changes fastest.
Arguments:
- density: float32 [2, 16, 64, 512], P('patch', None, 'theta', 'phi'), may hold values from 0.5 to 2
- velocity: float32 [2, 3, 16, 64, 512], P('patch', None, None, 'theta', 'phi'), may hold values from -3 to 3
- magnetic: float32 [2, 3, 16, 64, 512], P('patch', None, None, 'theta', 'phi'), may hold values from -3 to 3
- pressure: float32 [2, 16, 64, 512], P('patch', None, 'theta', 'phi'), may hold values from 0.5 to 2
- send_row: int32 [2, 4, 4, 144], P('patch', 'theta', 'phi'), may hold values from 0 to 14
- send_col: int32 [2, 4, 4, 144], P('patch', 'theta', 'phi'), may hold values from 0 to 126
- send_weight: float32 [2, 4, 4, 2, 144], P('patch', 'theta', 'phi'), may hold values from 0 to 1
- send_turn: float32 [2, 4, 4, 144], P('patch', 'theta', 'phi'), may hold values from -3.140625 to 3.140625
- send_dest: int32 [2, 4, 4, 144], P('patch', 'theta', 'phi'), may hold values from 0 to 1152, as said below
Outputs:
- new_density: float32 [2, 16, 64, 512], P('patch', None, 'theta', 'phi')
- new_velocity: float32 [2, 3, 16, 64, 512], P('patch', None, None, 'theta', 'phi')
- new_magnetic: float32 [2, 3, 16, 64, 512], P('patch', None, None, 'theta', 'phi')
- new_pressure: float32 [2, 16, 64, 512], P('patch', None, 'theta', 'phi')
Inputs may be any that keep to these rules, and one draw needn't show every extreme that they name: `send_dest`: each ghost point m < 1152 of a patch is named by exactly one slot of the other patch's tiles; unused slots hold 1152. Used slots lie only in tiles of the first and last tile rows and tile columns of a patch, and their donor cells lie within min(16, 128) cells of the patch's outer edge; the four corner tiles use all 144 slots, every other tile fewer.
All inputs are finite; a program needn't handle non-finite values.
Results may differ from a plain program's by a relative error of at most 0.00008.
Values sent between devices are 32-bit elements; how exact they have to be, the bound alone decides.
A program may use at most 64 MiB of HBM per device.

v0:
```python
import math

import jax
import jax.numpy as jnp
from jax import lax
from jax.sharding import PartitionSpec as P

GAMMA = 5.0 / 3.0
R_BASE = 0.6
DR_STEP = 0.65 / 64.0
COURANT = 0.4
DIFFUSE = 0.4


def with_halo(cells, sides, width):
    for axis, dim in sides:
        count = lax.axis_size(axis)
        ends = count - 1
        head = lax.slice_in_dim(cells, 0, width, axis=dim)
        tail = lax.slice_in_dim(cells, cells.shape[dim] - width, cells.shape[dim], axis=dim)
        cells = jnp.concatenate(
            [
                lax.ppermute(tail, axis, [(i, (i + 1) % count) for i in range(ends)]),
                cells,
                lax.ppermute(head, axis, [((i + 1) % count, i) for i in range(ends)]),
            ],
            axis=dim,
        )
    return cells


def grid_constants(total_theta, total_phi):
    d_theta = 0.5 * math.pi / total_theta
    d_phi = 1.5 * math.pi / total_phi
    r_low = R_BASE + 0.5 * DR_STEP
    inv_r = 1.0 / DR_STEP
    inv_t = 1.0 / (r_low * d_theta)
    inv_p = 1.0 / (r_low * math.sin(0.25 * math.pi) * d_phi)
    dt_step = COURANT / (inv_r + inv_t + inv_p)
    diffusivity = DIFFUSE / (dt_step * (inv_r * inv_r + inv_t * inv_t + inv_p * inv_p))
    return (d_theta, d_phi, dt_step, diffusivity)


def bilinear(low_low, low_high, high_low, high_high, weight_row, weight_col):
    return (1.0 - weight_row) * (
        (1.0 - weight_col) * low_low + weight_col * low_high
    ) + weight_row * ((1.0 - weight_col) * high_low + weight_col * high_high)


def turn_frame(blended, turn):
    cos_t = jnp.cos(turn)
    sin_t = jnp.sin(turn)
    flow_t = cos_t * blended[2] + sin_t * blended[3]
    flow_p = cos_t * blended[3] - sin_t * blended[2]
    field_t = cos_t * blended[5] + sin_t * blended[6]
    field_p = cos_t * blended[6] - sin_t * blended[5]
    return jnp.stack(
        [blended[0], blended[1], flow_t, flow_p, blended[4], field_t, field_p, blended[7]]
    )


def advance(padded, radius, sin_theta, d_theta, d_phi, dt_step, diffusivity):
    levels = padded.shape[1] - 2
    tile_rows = padded.shape[2] - 2
    tile_cols = padded.shape[3] - 2
    radial_h = 1.0 / DR_STEP
    colat_h = 1.0 / (radius[:, None, None] * d_theta)
    lon_h = 1.0 / (radius[:, None, None] * sin_theta[None, :, None] * d_phi)

    def shifted(field, step_r, step_t, step_p):
        return field[
            ...,
            1 + step_r : 1 + step_r + levels,
            1 + step_t : 1 + step_t + tile_rows,
            1 + step_p : 1 + step_p + tile_cols,
        ]

    def radial_diff(field):
        return (shifted(field, 1, 0, 0) - shifted(field, -1, 0, 0)) * (0.5 * radial_h)

    def colat_diff(field):
        return (shifted(field, 0, 1, 0) - shifted(field, 0, -1, 0)) * (0.5 * colat_h)

    def lon_diff(field):
        return (shifted(field, 0, 0, 1) - shifted(field, 0, 0, -1)) * (0.5 * lon_h)

    def laplace(field):
        centre = 2.0 * shifted(field, 0, 0, 0)
        return (
            (shifted(field, 1, 0, 0) + shifted(field, -1, 0, 0) - centre) * (radial_h * radial_h)
            + (shifted(field, 0, 1, 0) + shifted(field, 0, -1, 0) - centre) * (colat_h * colat_h)
            + (shifted(field, 0, 0, 1) + shifted(field, 0, 0, -1) - centre) * (lon_h * lon_h)
        )

    def cross_of(left_vec, right_vec):
        return jnp.stack(
            [
                left_vec[1] * right_vec[2] - left_vec[2] * right_vec[1],
                left_vec[2] * right_vec[0] - left_vec[0] * right_vec[2],
                left_vec[0] * right_vec[1] - left_vec[1] * right_vec[0],
            ]
        )

    def curl_of(field):
        return jnp.stack(
            [
                colat_diff(field[2]) - lon_diff(field[1]),
                lon_diff(field[0]) - radial_diff(field[2]),
                radial_diff(field[1]) - colat_diff(field[0]),
            ]
        )

    density_pad = padded[0]
    flow_pad = padded[1:4]
    magnet_pad = padded[4:7]
    press_pad = padded[7]
    density_c = shifted(density_pad, 0, 0, 0)
    flow_c = shifted(flow_pad, 0, 0, 0)
    magnet_c = shifted(magnet_pad, 0, 0, 0)
    press_c = shifted(press_pad, 0, 0, 0)
    momentum = density_pad[None] * flow_pad
    emf_pad = cross_of(flow_pad, magnet_pad)
    lorentz = cross_of(curl_of(magnet_pad), magnet_c)

    def carried(field):
        return (
            flow_c[0] * radial_diff(field)
            + flow_c[1] * colat_diff(field)
            + flow_c[2] * lon_diff(field)
        )

    div_mom = radial_diff(momentum[0]) + colat_diff(momentum[1]) + lon_diff(momentum[2])
    div_flow = radial_diff(flow_pad[0]) + colat_diff(flow_pad[1]) + lon_diff(flow_pad[2])
    press_grad = [radial_diff(press_pad), colat_diff(press_pad), lon_diff(press_pad)]
    new_density = density_c - dt_step * div_mom
    new_flow = jnp.stack(
        [
            flow_c[comp]
            + dt_step
            * (
                -carried(flow_pad[comp])
                + (lorentz[comp] - press_grad[comp]) / density_c
                + diffusivity * laplace(flow_pad[comp])
            )
            for comp in range(3)
        ]
    )
    new_magnet = magnet_c + dt_step * (curl_of(emf_pad) + diffusivity * laplace(magnet_pad))
    new_press = press_c + dt_step * (
        -carried(press_pad) - GAMMA * press_c * div_flow + diffusivity * laplace(press_pad)
    )
    return (new_density, new_flow, new_magnet, new_press)


def place_rows(target, wanted, values):
    hits = (target[:, None] == wanted[None, :]).astype(jnp.float32)
    return jnp.dot(
        hits.T, values, preferred_element_type=jnp.float32, precision=lax.Precision.HIGHEST
    )


def body(
    density, velocity, magnetic, pressure, send_row, send_col, send_weight, send_turn, send_dest
):
    fields = jnp.concatenate([density, velocity[0], magnetic[0], pressure], axis=0)
    levels = fields.shape[1]
    tile_rows = fields.shape[2]
    tile_cols = fields.shape[3]
    channels = 8 * levels
    theta_count = lax.axis_size("theta")
    phi_count = lax.axis_size("phi")
    total_theta = tile_rows * theta_count
    total_phi = tile_cols * phi_count
    d_theta, d_phi, dt_step, diffusivity = grid_constants(total_theta, total_phi)
    patch_index = lax.axis_index("patch")
    theta_index = lax.axis_index("theta")
    phi_index = lax.axis_index("phi")
    flattened = fields.reshape(channels, tile_rows * tile_cols)
    base_cell = send_row.reshape(-1) * tile_cols + send_col.reshape(-1)

    def corner(offset):
        return jnp.take(flattened, base_cell + offset, axis=1).reshape(8, levels, -1)

    weights = send_weight.reshape(2, -1)
    blended = bilinear(
        corner(0), corner(1), corner(tile_cols), corner(tile_cols + 1), weights[0], weights[1]
    )
    donor_rows = turn_frame(blended, send_turn.reshape(-1)).reshape(channels, -1).T
    target = send_dest.reshape(-1)
    lon_values = lax.all_gather(donor_rows, "phi", axis=0, tiled=True)
    lon_targets = lax.all_gather(target, "phi", axis=0, tiled=True)
    own_lon = phi_index * tile_cols + jnp.arange(tile_cols, dtype=jnp.int32)
    lon_part = jnp.concatenate(
        [
            place_rows(lon_targets, own_lon, lon_values),
            place_rows(lon_targets, own_lon + total_phi, lon_values),
        ],
        axis=1,
    )
    lat_ids = jnp.arange(total_theta, dtype=jnp.int32) + 2 * total_phi
    lat_full = jnp.concatenate(
        [
            place_rows(target, lat_ids, donor_rows),
            place_rows(target, lat_ids + total_theta, donor_rows),
        ],
        axis=1,
    )
    lat_part = lax.psum_scatter(lat_full, "theta", scatter_dimension=0, tiled=True)
    slot_mask = (jnp.arange(2, dtype=jnp.int32) == 1 - patch_index)[:, None, None]
    lon_total = lax.psum(jnp.where(slot_mask, lon_part[None], 0.0), ("patch", "theta"))
    lat_total = lax.psum(jnp.where(slot_mask, lat_part[None], 0.0), ("patch", "phi"))
    lon_border = lax.dynamic_index_in_dim(lon_total, patch_index, 0, keepdims=False)
    lat_border = lax.dynamic_index_in_dim(lat_total, patch_index, 0, keepdims=False)
    upper_side = lon_border[:, :channels].T.reshape(8, levels, tile_cols)
    lower_side = lon_border[:, channels:].T.reshape(8, levels, tile_cols)
    left_side = lat_border[:, :channels].T.reshape(8, levels, tile_rows)
    right_side = lat_border[:, channels:].T.reshape(8, levels, tile_rows)
    rims = with_halo(fields, (("theta", 2), ("phi", 3)), 1)
    padded = jnp.pad(rims, ((0, 0), (1, 1), (0, 0), (0, 0)), mode="edge")
    padded = padded.at[:, 1:-1, 0, 1:-1].set(
        jnp.where(theta_index == 0, upper_side, padded[:, 1:-1, 0, 1:-1])
    )
    padded = padded.at[:, 1:-1, -1, 1:-1].set(
        jnp.where(theta_index == theta_count - 1, lower_side, padded[:, 1:-1, -1, 1:-1])
    )
    padded = padded.at[:, 1:-1, 1:-1, 0].set(
        jnp.where(phi_index == 0, left_side, padded[:, 1:-1, 1:-1, 0])
    )
    padded = padded.at[:, 1:-1, 1:-1, -1].set(
        jnp.where(phi_index == phi_count - 1, right_side, padded[:, 1:-1, 1:-1, -1])
    )
    radius = R_BASE + (jnp.arange(levels, dtype=jnp.float32) + 0.5) * DR_STEP
    rows_global = theta_index * tile_rows + jnp.arange(tile_rows, dtype=jnp.int32)
    sin_theta = jnp.sin(0.25 * math.pi + (rows_global.astype(jnp.float32) + 0.5) * d_theta)
    new_density, new_flow, new_magnet, new_press = advance(
        padded, radius, sin_theta, d_theta, d_phi, dt_step, diffusivity
    )
    return (new_density[None], new_flow[None], new_magnet[None], new_press[None])


def solution(mesh):
    placed = (
        P("patch", None, "theta", "phi"),
        P("patch", None, None, "theta", "phi"),
        P("patch", None, None, "theta", "phi"),
        P("patch", None, "theta", "phi"),
        P("patch", "theta", "phi", None),
        P("patch", "theta", "phi", None),
        P("patch", "theta", "phi", None, None),
        P("patch", "theta", "phi", None),
        P("patch", "theta", "phi", None),
    )
    return jax.shard_map(
        body,
        mesh=mesh,
        in_specs=placed,
        out_specs=(
            P("patch", None, "theta", "phi"),
            P("patch", None, None, "theta", "phi"),
            P("patch", None, None, "theta", "phi"),
            P("patch", None, "theta", "phi"),
        ),
        check_vma=False,
    )
```

profile of v0, /device:TPU:0, one launch (start us, length us, event | category | flops | bytes accessed | tf_op | source)
XLA Modules:
  0.0 169.6 jit_solution(17731165187962322360)
XLA Ops:
  8.0 0.7 multiply_add_fusion.1
  8.8 1.0 copy.88
  9.8 1.0 copy.89
  10.8 1.4 copy_bitcast_fusion.1
  12.9 1.3 copy.147
  14.2 1.5 copy.95
  15.8 0.7 gather_fusion.1
  16.7 0.7 gather_fusion.2
  17.5 0.7 copy.100
  18.2 0.7 gather_fusion.3
  19.0 0.7 copy.102
  20.6 1.0 multiply_add_fusion
  23.2 5.0 %collective-permute-start = (f32[8,16,1,128]{3,1,0,2:T(8,128)S(1)}, f32[8,16,1,128]{3,1,0,2:T(8,128)S(1)}, u32[]{:S(2)}, u32[]{:S(2)}) collective-permute-start(f32[8,16,1,128]{3,1,0,2:T(8,128)S(1)} %get-tuple-element.88), channel_id=1, source_target_pairs={{0,4},{4,8},{8,12},{1,5},{5,9},{9,13},{2,6},{6,10},{10,14},{3,7},{... | collective-permute-start | bytes 196616 | tf_op jit(solution)/shard_map/ppermute | solution.py:23
  28.1 1.3 collective-permute-start.1
  29.6 9.1 %all_gather.7 = f32[576,128]{1,0:T(8,128)S(1)} all-gather(f32[144,128]{1,0:T(8,128)S(1)} %copy.103), channel_id=1, replica_groups=mesh['patch'=2,'theta'=4,'phi'=4] {'phi'}, dimensions={0}, use_global_device_ids=true | all-gather | bytes 368640 | tf_op jit(solution)/shard_map/all_gather | solution.py:190
  38.7 1.3 dynamic-slice.36
  41.0 7.6 %all-reduce = s32[576]{0:T(1024)S(1)} all-reduce(s32[576]{0:T(1024)S(1)} %dynamic-update-slice.12), channel_id=2, replica_groups=mesh['patch'=2,'theta'=4,'phi'=4] {'phi'}, use_global_device_ids=true, to_apply=%add | all-reduce | flops 576 | bytes 4608
  49.7 0.8 broadcast_select_fusion
  51.2 1.5 copy.90
  52.7 2.2 %collective-permute-start.2 = (f32[8,16,18,1]{2,1,3,0:T(8,128)}, f32[8,16,18,1]{2,1,3,0:T(8,128)S(1)}, u32[]{:S(2)}, u32[]{:S(2)}) collective-permute-start(f32[8,16,18,1]{2,1,3,0:T(8,128)} %copy.90), channel_id=1, source_target_pairs={{0,1},{1,2},{2,3},{4,5},{5,6},{6,7},{8,9},{9,10},{10,11},{12,13},{... | collective-permute-start | bytes 27656 | tf_op jit(solution)/shard_map/ppermute | solution.py:23
  54.9 0.9 copy.91
  55.8 1.5 collective-permute-start.3
  57.9 1.3 copy.92
  59.2 2.9 %collective-permute-done.3 = f32[8,16,18,1]{2,1,3,0:T(8,128)} collective-permute-done((f32[8,16,18,1]{2,1,3,0:T(8,128)S(1)}, f32[8,16,18,1]{2,1,3,0:T(8,128)}, u32[]{:S(2)}, u32[]{:S(2)}) %collective-permute-start.3) | collective-permute-done | bytes 9248 | tf_op jit(solution)/shard_map/ppermute | solution.py:25
  62.1 2.1 %copy.93 = f32[8,16,18,1]{3,1,0,2:T(8,128)S(1)} copy(f32[8,16,18,1]{2,1,3,0:T(8,128)} %collective-permute-done.3) | data formatting | bytes 18432 | tf_op jit(solution)/shard_map/ppermute | solution.py:25
  64.3 1.0 pad_maximum_fusion.1
  65.5 5.2 %pad_maximum_fusion = f32[8,18,18,130]{3,1,0,2:T(8,128)S(1)} fusion(f32[8,1,18,130]{3,1,0,2:T(1,128)S(1)} %get-tuple-element.82, f32[8,16,18,1]{3,1,0,2:T(8,128)} %copy-done.1, f32[8,16,1,128]{3,1,0,2:T(8,128)} %copy-done.7, f32[1,16,16,128]{3,1,0,2:T(8,128)} %copy-done.5, f32[3,16,16,128]{3,1,0,2:T(8,128)} %copy-done.2, f32[3,16,16,128]{3,1,0,2:T(8,128)} %copy-done.3, ...), kind=kLoop, calls=%fused_computation.4 | loop fusion | flops 3032640 | bytes 2695680 | tf_op jit(solution)/shard_map/jit(_pad)/concatenate | solution.py:219
  70.8 1.4 broadcast_select_fusion.2
  72.2 28.6 %psum.15 = f32[2,16,256]{2,1,0:T(8,128)} all-reduce(f32[2,16,256]{2,1,0:T(8,128)} %broadcast_select_fusion.2), channel_id=1, replica_groups=mesh['patch'=2,'theta'=4,'phi'=4] {'patch','phi'}, use_global_device_ids=true, to_apply=%region_2.4 | all-reduce | flops 8192 | bytes 65536 | tf_op jit(solution)/shard_map/psum | solution.py:211
  100.8 0.7 dynamic-slice_bitcast_fusion.1
  102.1 2.6 %reshape.506 = f32[8,16,16,1]{3,1,0,2:T(8,128)} reshape(f32[128,16]{0,1:T(8,128)} %get-tuple-element.96) | data formatting | bytes 16384 | tf_op jit(solution)/shard_map/reshape | solution.py:216
  104.7 2.7 %all-reduce.3.cloned.1.call-done = f32[2,128,256]{1,2,0:T(8,128)} async-done(((f32[2,128,256]{1,2,0:T(8,128)}), f32[2,128,256]{1,2,0:T(8,128)}) %all-reduce.3.cloned.1.call-update) | async-done | bytes 262160 | tf_op jit(solution)/shard_map/psum | solution.py:210
  107.4 0.9 dynamic-slice_bitcast_fusion
  109.5 3.7 %scatter.14 = f32[8,18,18,130]{3,1,0,2:T(8,128)S(1)} dynamic-update-slice(f32[8,18,18,130]{3,1,0,2:T(8,128)S(1)} %pad_maximum_fusion, f32[8,16,1,128]{3,1,0,2:T(8,128)} %broadcast_select_fusion.1, s32[]{:T(128)} %constant.196.clone.1, s32[]{:T(128)} %constant.197.clone.1, s32[]{:T(128)} %constant.196.clone.1, s32[]{:T(128)} %constant.197.clone.1) | dynamic-update-slice | bytes 131076 | tf_op jit(solution)/shard_map/scatter | solution.py:220
  113.2 0.7 slice_select_fusion.2
  114.0 3.7 %scatter.15 = f32[8,18,18,130]{3,1,0,2:T(8,128)S(1)} dynamic-update-slice(f32[8,18,18,130]{3,1,0,2:T(8,128)S(1)} %scatter.14, f32[8,16,1,128]{3,1,0,2:T(8,128)} %slice_select_fusion.2, s32[]{:T(128)} %constant.196.clone.1, s32[]{:T(128)} %constant.197.clone.1, s32[]{:T(128)} %constant.207.clone.1, s32[]{:T(128)} %constant.197.clone.1) | dynamic-update-slice | bytes 131076 | tf_op jit(solution)/shard_map/scatter | solution.py:223
  117.7 2.4 %slice_select_fusion.1 = f32[8,16,16,1]{3,1,0,2:T(8,128)} fusion(f32[8,16,16,1]{3,1,0,2:T(8,128)} %reshape.506, f32[8,18,18,130]{3,1,0,2:T(8,128)S(1)} %scatter.15, pred[]{:T(512)S(6)} %eq.79), kind=kLoop, calls=%fused_computation.10 | loop fusion | flops 2048 | bytes 24577 | tf_op jit(solution)/shard_map/jit(_where)/select_n | solution.py:227
  120.1 6.1 %scatter.16 = f32[8,18,18,130]{3,1,0,2:T(8,128)S(1)} dynamic-update-slice(f32[8,18,18,130]{3,1,0,2:T(8,128)S(1)} %scatter.15, f32[8,16,16,1]{3,1,0,2:T(8,128)} %slice_select_fusion.1, s32[]{:T(128)} %constant.196.clone.1, s32[]{:T(128)} %constant.197.clone.1, s32[]{:T(128)} %constant.197.clone.1, s32[]{:T(128)} %constant.196.clone.1) | dynamic-update-slice | bytes 16388 | tf_op jit(solution)/shard_map/scatter | solution.py:226
  126.2 2.6 %reshape.507 = f32[8,16,16,1]{3,1,0,2:T(8,128)} reshape(f32[128,16]{0,1:T(8,128)} %get-tuple-element.95) | data formatting | bytes 16384 | tf_op jit(solution)/shard_map/reshape | solution.py:217
  128.8 1.3 slice_select_fusion
  130.1 23.2 %scatter.19 = f32[8,18,18,130]{3,1,0,2:T(8,128)S(1)} dynamic-update-slice(f32[8,18,18,130]{3,1,0,2:T(8,128)S(1)} %scatter.16, f32[8,16,16,1]{3,1,0,2:T(8,128)} %slice_select_fusion, s32[]{:T(128)} %constant.196.clone.1, s32[]{:T(128)} %constant.197.clone.1, s32[]{:T(128)} %constant.197.clone.1, s32[]{:T(128)} %constant.202.clone.1) | dynamic-update-slice | bytes 16388 | tf_op jit(solution)/shard_map/scatter | solution.py:229
  155.0 0.7 copy.126
  156.1 0.7 fusion.7
  156.9 0.9 copy.125
  157.9 0.9 add_bitcast_fusion.3
  158.7 0.7 add_bitcast_fusion.2
  160.1 0.9 copy.124
  161.4 0.7 copy.123
  (91 shorter events, 11.6 us)
Async XLA Ops:
  8.0 62.8 %reduce-scatter.2.cloned.1.call-start = ((), (), s32[]{:S(2)}) async-start(), calls=%async_computation.2 | async-start | bytes 81920 | tf_op jit(solution)/shard_map/reduce_scatter | solution.py:208
  9.7 54.5 %copy-start.4 = (f32[1,16,16,128]{3,1,0,2:T(8,128)}, f32[1,16,16,128]{3,1,0,2:T(8,128)S(1)}, u32[]{:S(2)}) copy-start(f32[1,16,16,128]{3,1,0,2:T(8,128)S(1)} %copy.88) | copy-start | bytes 393220
  10.8 53.5 %copy-start.5 = (f32[1,16,16,128]{3,1,0,2:T(8,128)}, f32[1,16,16,128]{3,1,0,2:T(8,128)S(1)}, u32[]{:S(2)}) copy-start(f32[1,16,16,128]{3,1,0,2:T(8,128)S(1)} %copy.89) | copy-start | bytes 393220
  12.2 52.1 %copy-start.2 = (f32[3,16,16,128]{3,1,0,2:T(8,128)}, f32[3,16,16,128]{3,1,0,2:T(8,128)S(1)}, u32[]{:S(2)}) copy-start(f32[3,16,16,128]{3,1,0,2:T(8,128)S(1)} %get-tuple-element.111) | copy-start | bytes 1179652
  12.2 52.1 %copy-start.3 = (f32[3,16,16,128]{3,1,0,2:T(8,128)}, f32[3,16,16,128]{3,1,0,2:T(8,128)S(1)}, u32[]{:S(2)}) copy-start(f32[3,16,16,128]{3,1,0,2:T(8,128)S(1)} %get-tuple-element.112) | copy-start | bytes 1179652
  16.7 3.9 %copy-start.12 = (f32[1,1,1,2,144]{4,3,2,1,0:T(2,128)S(1)}, f32[1,1,1,2,144]{4,3,2,1,0:T(2,128)}, u32[]{:S(2)}) copy-start(f32[1,1,1,2,144]{4,3,2,1,0:T(2,128)} %param.25) | copy-start | bytes 3460
  17.4 4.3 %copy-start.13 = (f32[1,1,1,144]{3,2,1,0:T(1,128)S(1)}, f32[1,1,1,144]{3,2,1,0:T(1,128)}, u32[]{:S(2)}) copy-start(f32[1,1,1,144]{3,2,1,0:T(1,128)} %param.26) | copy-start | bytes 1732
  17.4 4.4 %copy-start.10 = (s32[1,1,1,144]{3,2,1,0:T(1,128)S(1)}, s32[1,1,1,144]{3,2,1,0:T(1,128)}, u32[]{:S(2)}) copy-start(s32[1,1,1,144]{3,2,1,0:T(1,128)} %param.27) | copy-start | bytes 1732
  23.1 84.3 %all-reduce.3.cloned.1.call-start = ((), (), s32[]{:S(2)}) async-start(), calls=%async_computation.1 | async-start | bytes 524288 | tf_op jit(solution)/shard_map/psum | solution.py:210
  23.2 27.4 %collective-permute-start = (f32[8,16,1,128]{3,1,0,2:T(8,128)S(1)}, f32[8,16,1,128]{3,1,0,2:T(8,128)S(1)}, u32[]{:S(2)}, u32[]{:S(2)}) collective-permute-start(f32[8,16,1,128]{3,1,0,2:T(8,128)S(1)} %get-tuple-element.88), channel_id=1, source_target_pairs={{0,4},{4,8},{8,12},{1,5},{5,9},{9,13},{2,6},{6,10},{10,14},{3,7},{... | collective-permute-start | bytes 196616 | tf_op jit(solution)/shard_map/ppermute | solution.py:23
  28.1 22.5 %collective-permute-start.1 = (f32[8,16,1,128]{3,1,0,2:T(8,128)S(1)}, f32[8,16,1,128]{3,1,0,2:T(8,128)S(1)}, u32[]{:S(2)}, u32[]{:S(2)}) collective-permute-start(f32[8,16,1,128]{3,1,0,2:T(8,128)S(1)} %get-tuple-element.89), channel_id=1, source_target_pairs={{4,0},{8,4},{12,8},{5,1},{9,5},{13,9},{6,2},{10,6},{14,10},{7,3},{... | collective-permute-start | bytes 196616 | tf_op jit(solution)/shard_map/ppermute | solution.py:25
  29.5 21.2 %copy-start.11 = (pred[2]{0:T(512)(128)(4,1)}, pred[2]{0:T(512)(128)(4,1)S(1)}, u32[]{:S(2)}) copy-start(pred[2]{0:T(512)(128)(4,1)S(1)} %iota_compare_fusion) | copy-start | bytes 10
  50.6 13.7 %copy-start.6 = (f32[8,16,1,128]{3,1,0,2:T(8,128)}, f32[8,16,1,128]{3,1,0,2:T(8,128)S(1)}, u32[]{:S(2)}) copy-start(f32[8,16,1,128]{3,1,0,2:T(8,128)S(1)} %collective-permute-done) | copy-start | bytes 196612
  50.6 13.7 %copy-start.7 = (f32[8,16,1,128]{3,1,0,2:T(8,128)}, f32[8,16,1,128]{3,1,0,2:T(8,128)S(1)}, u32[]{:S(2)}) copy-start(f32[8,16,1,128]{3,1,0,2:T(8,128)S(1)} %collective-permute-done.1) | copy-start | bytes 196612
  52.7 5.2 %collective-permute-start.2 = (f32[8,16,18,1]{2,1,3,0:T(8,128)}, f32[8,16,18,1]{2,1,3,0:T(8,128)S(1)}, u32[]{:S(2)}, u32[]{:S(2)}) collective-permute-start(f32[8,16,18,1]{2,1,3,0:T(8,128)} %copy.90), channel_id=1, source_target_pairs={{0,1},{1,2},{2,3},{4,5},{5,6},{6,7},{8,9},{9,10},{10,11},{12,13},{... | collective-permute-start | bytes 27656 | tf_op jit(solution)/shard_map/ppermute | solution.py:23
  55.8 6.3 %collective-permute-start.3 = (f32[8,16,18,1]{2,1,3,0:T(8,128)S(1)}, f32[8,16,18,1]{2,1,3,0:T(8,128)}, u32[]{:S(2)}, u32[]{:S(2)}) collective-permute-start(f32[8,16,18,1]{2,1,3,0:T(8,128)S(1)} %copy.91), channel_id=1, source_target_pairs={{1,0},{2,1},{3,2},{5,4},{6,5},{7,6},{9,8},{10,9},{11,10},{13,12},{... | collective-permute-start | bytes 27656 | tf_op jit(solution)/shard_map/ppermute | solution.py:25
  59.2 6.1 %copy-start = (f32[8,16,18,1]{3,1,0,2:T(8,128)}, f32[8,16,18,1]{3,1,0,2:T(8,128)S(1)}, u32[]{:S(2)}) copy-start(f32[8,16,18,1]{3,1,0,2:T(8,128)S(1)} %copy.92) | copy-start | bytes 27652
  64.3 1.0 copy-start.1
  153.7 0.7 copy-start.8
  153.7 0.7 copy-start.9
Sparse Core Ops, SparseCore 0:
  23.2 22.0 reduce-scatter.1
Sparse Core Ops, SparseCore 1:
  50.5 56.7 all-reduce.2
where the time goes:
time: 171 us; the launch traced here: 170 us
  local copies, waits for them, and re-layouts  68.2 us (40%)
  blocking collectives  45.3 us (26%)
  other arithmetic  21.8 us (13%)
  between operations  16.9 us (10%)
  starting transfers between devices  10 us (6%)
  waiting for transfers between devices  5.58 us (3%)
  matrix products  1.73 us (1%)
    psum x1, blocking collectives, body(): lax.psum(jnp.where(slot_mask, lat_part[None], 0.0), ('patch', 'phi'))  28.6 us
    scatter x1, local copies, waits for them, and re-layouts, body(): padded.at[:, 1:-1, 1:-1, -1]  23.2 us
    all_gather x1, blocking collectives, body(): lon_values = lax.all_gather(donor_rows, 'phi', axis=0, tiled=True)  9.12 us
    unnamed x40, local copies, waits for them, and re-layouts  8.56 us
    unnamed x1, blocking collectives  7.56 us
    ppermute x2, starting transfers between devices, with_halo(): lax.ppermute(tail, axis, [(i, (i + 1) % count) for i in range(ends)])  7.18 us
    scatter x1, local copies, waits for them, and re-layouts, body(): padded.at[:, 1:-1, 1:-1, 0]  6.14 us
    concatenate x1, other arithmetic, body(): padded = jnp.pad(rims, ((0, 0), (1, 1), (0, 0), (0, 0)), mode='edge')  5.19 us
  transfers between devices with their start and end apart: 6, of which 2 were waited for; matrix products, arithmetic and copies ran while one was open for 13% of the time, Pallas kernels for 0%

commit v1 on v0

v1 whole, which is shorter than its diff:
```python
import functools
import math

import jax
import jax.numpy as jnp
import numpy as np
from jax import lax
from jax.experimental import pallas as pl
from jax.experimental.pallas import tpu as pltpu
from jax.sharding import PartitionSpec as P

GAMMA = 5.0 / 3.0
R_BASE = 0.6
DR_STEP = 0.65 / 64.0
COURANT = 0.4
DIFFUSE = 0.4
MESH = pl.DeviceIdType.MESH
LANES = 128
HEAD = 8


def grid_constants(total_theta, total_phi):
    d_theta = 0.5 * math.pi / total_theta
    d_phi = 1.5 * math.pi / total_phi
    r_low = R_BASE + 0.5 * DR_STEP
    inv_r = 1.0 / DR_STEP
    inv_t = 1.0 / (r_low * d_theta)
    inv_p = 1.0 / (r_low * math.sin(0.25 * math.pi) * d_phi)
    dt_step = COURANT / (inv_r + inv_t + inv_p)
    diffusivity = DIFFUSE / (dt_step * (inv_r * inv_r + inv_t * inv_t + inv_p * inv_p))
    return (d_theta, d_phi, dt_step, diffusivity)


def split(x):
    hi = x.astype(jnp.bfloat16)
    lo = (x - hi.astype(jnp.float32)).astype(jnp.bfloat16)
    return hi, lo


def dot_nt(a, b):
    return lax.dot_general(a, b, (((1,), (1,)), ((), ())), preferred_element_type=jnp.float32)


def dot_nn(a, b):
    return jnp.dot(a, b, preferred_element_type=jnp.float32)


def exchange_kernel(
    dims, den, vel, mag, prs, srow, scol, swgt, sturn, sdest,
    up_out, down_out, left_out, right_out,
    table, gathered, rows_out, rows_in, cols_out, cols_in, lon_out, lon_in, lat_out, lat_in,
    gather_send, gather_recv, lon_send, lon_recv, lat_send, lat_recv, halo_send, halo_recv,
):
    n_theta, n_phi, levels, tile_rows, tile_cols, slots = dims
    total_phi = tile_cols * n_phi
    total_theta = tile_rows * n_theta
    channels = 8 * levels
    chunks = -(-slots // LANES)
    q = lax.axis_index("patch")
    t = lax.axis_index("theta")
    f = lax.axis_index("phi")
    other = 1 - q

    barrier = pltpu.get_barrier_semaphore()

    def greet(device):
        pl.semaphore_signal(barrier, inc=1, device_id=device, device_id_type=MESH)

    for d in range(1, n_phi):
        greet((q, t, lax.rem(f + d, n_phi)))
    greet((q, lax.rem(t + 1, n_theta), f))
    greet((q, lax.rem(t + n_theta - 1, n_theta), f))
    for d in range(n_theta):
        greet((other, d, f))

    table[...] = jnp.zeros_like(table)
    table[0:1, :slots] = srow[...].astype(jnp.float32)
    table[1:2, :slots] = scol[...].astype(jnp.float32)
    table[2:4, :slots] = swgt[...]
    turn = sturn[...]
    table[4:5, :slots] = jnp.cos(turn)
    table[5:6, :slots] = jnp.sin(turn)
    dest_row = sdest[...].astype(jnp.float32)
    table[6:7, :slots] = dest_row
    columns = table[...].T[:slots]
    row_s = columns[:, 0:1]
    col_s = columns[:, 1:2]
    w_row = columns[:, 2:3]
    w_col = columns[:, 3:4]
    cos_s = columns[:, 4:5]
    sin_s = columns[:, 5:6]

    lane = lax.broadcasted_iota(jnp.int32, (slots, tile_cols), 1).astype(jnp.float32)
    pick = jnp.where(lane == col_s, 1.0 - w_col, 0.0) + jnp.where(lane == col_s + 1.0, w_col, 0.0)
    pick_hi, pick_lo = split(pick)

    def field_row(r):
        return jnp.concatenate(
            [
                den[pl.ds(r, levels, stride=tile_rows), :],
                vel[pl.ds(r, 3 * levels, stride=tile_rows), :],
                mag[pl.ds(r, 3 * levels, stride=tile_rows), :],
                prs[pl.ds(r, levels, stride=tile_rows), :],
            ],
            axis=0,
        )

    value = jnp.zeros((slots, channels), jnp.float32)
    for r in range(tile_rows):
        cells = field_row(r)
        if r == 0:
            rows_out[0] = cells
        if r == tile_rows - 1:
            rows_out[1] = cells
        hi, lo = split(cells)
        part = dot_nt(pick_hi, hi) + (dot_nt(pick_hi, lo) + dot_nt(pick_lo, hi))
        gain = jnp.where(row_s == r, 1.0 - w_row, 0.0) + jnp.where(row_s + 1.0 == r, w_row, 0.0)
        value = value + gain * part
    comp = lax.broadcasted_iota(jnp.int32, (slots, channels), 1) // levels
    first = (comp == 2) | (comp == 5)
    second = (comp == 3) | (comp == 6)
    partner = jnp.where(
        first,
        pltpu.roll(value, channels - levels, axis=1),
        pltpu.roll(value, levels, axis=1),
    )
    keep = jnp.where(first | second, cos_s, 1.0)
    mix = jnp.where(first, sin_s, jnp.where(second, -sin_s, 0.0))
    own = gathered.at[f]
    own[HEAD:HEAD + slots, :] = keep * value + mix * partner
    for c in range(chunks):
        own[c:c + 1, :] = table[6:7, c * LANES:(c + 1) * LANES]

    pl.semaphore_wait(barrier, n_phi - 1 + 2 + n_theta)

    def gather_copy(d):
        return pltpu.make_async_remote_copy(
            src_ref=gathered.at[f],
            dst_ref=gathered.at[f],
            send_sem=gather_send.at[d - 1],
            recv_sem=gather_recv.at[d - 1],
            device_id=(q, t, lax.rem(f + d, n_phi)),
            device_id_type=MESH,
        )

    for d in range(1, n_phi):
        gather_copy(d).start()

    def row_copy(way):
        return pltpu.make_async_remote_copy(
            src_ref=rows_out.at[way],
            dst_ref=rows_in.at[way],
            send_sem=halo_send.at[way],
            recv_sem=halo_recv.at[way],
            device_id=(q, lax.rem(t + (1 if way else n_theta - 1), n_theta), f),
            device_id_type=MESH,
        )

    def col_copy(way):
        return pltpu.make_async_remote_copy(
            src_ref=cols_out.at[way],
            dst_ref=cols_in.at[way],
            send_sem=halo_send.at[2 + way],
            recv_sem=halo_recv.at[2 + way],
            device_id=(q, t, lax.rem(f + (1 if way else n_phi - 1), n_phi)),
            device_id_type=MESH,
        )

    @pl.when(t > 0)
    def _():
        row_copy(0).start()

    @pl.when(t < n_theta - 1)
    def _():
        row_copy(1).start()

    lane2 = lax.broadcasted_iota(jnp.int32, (tile_rows, channels), 1)
    low = jnp.zeros((tile_rows, channels), jnp.float32)
    high = jnp.zeros((tile_rows, channels), jnp.float32)
    for c in range(8):
        ref, base = ((den, 0), (vel, 0), (vel, 1), (vel, 2), (mag, 0), (mag, 1), (mag, 2), (prs, 0))[c]
        for k in range(levels):
            cells = ref[(base * levels + k) * tile_rows:(base * levels + k + 1) * tile_rows, :]
            hit = lane2 == c * levels + k
            low = jnp.where(hit, cells[:, 0:1], low)
            high = jnp.where(hit, cells[:, tile_cols - 1:tile_cols], high)
    cols_out[0] = low
    cols_out[1] = high

    def ids_of(count):
        return lax.broadcasted_iota(jnp.int32, (count, LANES), 0)

    ids_top = ids_of(tile_cols) + f * tile_cols
    lat_base = 2 * total_phi + jnp.where(f == 0, 0, total_theta)
    ids = jnp.concatenate(
        [ids_top, ids_top + total_phi, ids_of(total_theta) + lat_base], axis=0
    ).astype(jnp.float32)

    def place(slot_ref):
        total = None
        for c in range(chunks):
            size = min(LANES, slots - c * LANES)
            hits = jnp.where(ids == slot_ref[c:c + 1, :], 1.0, 0.0).astype(jnp.bfloat16)
            hi, lo = split(slot_ref[HEAD + c * LANES:HEAD + c * LANES + size, :])
            hits = hits[:, :size]
            term = dot_nn(hits, hi) + dot_nn(hits, lo)
            total = term if total is None else total + term
        return total

    @pl.when(f > 0)
    def _():
        col_copy(0).start()

    @pl.when(f < n_phi - 1)
    def _():
        col_copy(1).start()

    placed = place(gathered.at[f])
    for d in range(1, n_phi):
        source = lax.rem(f + n_phi - d, n_phi)
        pltpu.make_async_remote_copy(
            src_ref=gathered.at[source],
            dst_ref=gathered.at[source],
            send_sem=gather_send.at[d - 1],
            recv_sem=gather_recv.at[d - 1],
            device_id=(q, t, source),
            device_id_type=MESH,
        ).wait_recv()
        placed = placed + place(gathered.at[source])
    lon_out[0] = placed[:tile_cols]
    lon_out[1] = placed[tile_cols:2 * tile_cols]
    lat_out[...] = placed[2 * tile_cols:]

    def lon_copy(side):
        return pltpu.make_async_remote_copy(
            src_ref=lon_out.at[side],
            dst_ref=lon_in.at[t],
            send_sem=lon_send.at[side],
            recv_sem=lon_recv.at[t],
            device_id=(other, (n_theta - 1) * side, f),
            device_id_type=MESH,
        )

    def lat_copy(d):
        return pltpu.make_async_remote_copy(
            src_ref=lat_out.at[pl.ds(d * tile_rows, tile_rows)],
            dst_ref=lat_in.at[t],
            send_sem=lat_send.at[d],
            recv_sem=lat_recv.at[t],
            device_id=(other, d, f),
            device_id_type=MESH,
        )

    lon_copy(0).start()
    lon_copy(1).start()

    at_side = (f == 0) | (f == n_phi - 1)
    at_end = (t == 0) | (t == n_theta - 1)

    @pl.when(at_side)
    def _():
        for d in range(n_theta):
            lat_copy(d).start()

    @pl.when(t > 0)
    def _():
        row_copy(1).wait_recv()
        up_out[...] = rows_in[1]

    @pl.when(t < n_theta - 1)
    def _():
        row_copy(0).wait_recv()
        down_out[...] = rows_in[0]

    @pl.when(f > 0)
    def _():
        col_copy(1).wait_recv()
        left_out[...] = cols_in[1]

    @pl.when(f < n_phi - 1)
    def _():
        col_copy(0).wait_recv()
        right_out[...] = cols_in[0]

    @pl.when(at_end)
    def _():
        for s in range(n_theta):
            pltpu.make_async_remote_copy(
                src_ref=lon_in.at[s],
                dst_ref=lon_in.at[s],
                send_sem=lon_send.at[0],
                recv_sem=lon_recv.at[s],
                device_id=(other, s, f),
                device_id_type=MESH,
            ).wait_recv()
        total = lon_in[0]
        for s in range(1, n_theta):
            total = total + lon_in[s]
        total = total.T

        @pl.when(t == 0)
        def _():
            up_out[...] = total

        @pl.when(t == n_theta - 1)
        def _():
            down_out[...] = total

    @pl.when(at_side)
    def _():
        for s in range(n_theta):
            pltpu.make_async_remote_copy(
                src_ref=lat_in.at[s],
                dst_ref=lat_in.at[s],
                send_sem=lat_send.at[0],
                recv_sem=lat_recv.at[s],
                device_id=(other, s, f),
                device_id_type=MESH,
            ).wait_recv()
        total = lat_in[0]
        for s in range(1, n_theta):
            total = total + lat_in[s]

        @pl.when(f == 0)
        def _():
            left_out[...] = total

        @pl.when(f == n_phi - 1)
        def _():
            right_out[...] = total

    for d in range(1, n_phi):
        gather_copy(d).wait_send()
    lon_copy(0).wait_send()
    lon_copy(1).wait_send()

    @pl.when(at_side)
    def _():
        for d in range(n_theta):
            lat_copy(d).wait_send()

    @pl.when(t > 0)
    def _():
        row_copy(0).wait_send()

    @pl.when(t < n_theta - 1)
    def _():
        row_copy(1).wait_send()

    @pl.when(f > 0)
    def _():
        col_copy(0).wait_send()

    @pl.when(f < n_phi - 1)
    def _():
        col_copy(1).wait_send()


def stencil_kernel(
    dims, den, vel, mag, prs, up, down, left, right, metric, inv_radius,
    new_den, new_vel, new_mag, new_prs,
):
    n_theta, n_phi, levels, rows, cols, _ = dims
    d_theta, _, dt_step, diffusivity = grid_constants(rows * n_theta, cols * n_phi)
    g_r = 1.0 / DR_STEP
    first_row = pl.multiple_of(lax.axis_index("theta") * rows, rows)
    lon_row = metric[pl.ds(first_row, rows), :]
    row_id = lax.broadcasted_iota(jnp.int32, (rows, cols), 0)
    col_id = lax.broadcasted_iota(jnp.int32, (rows, cols), 1)
    at_up = row_id == 0
    at_down = row_id == rows - 1
    at_left = col_id == 0
    at_right = col_id == cols - 1
    sources = ((den, 0), (vel, 0), (vel, 1), (vel, 2), (mag, 0), (mag, 1), (mag, 2), (prs, 0))
    channels = 8 * levels

    def level(k, carry):
        inv_rk = inv_radius[k]
        g_t = inv_rk * (1.0 / d_theta)
        g_p = lon_row * inv_rk
        half_r = 0.5 * g_r
        half_t = 0.5 * g_t
        half_p = 0.5 * g_p
        below = jnp.maximum(k - 1, 0)
        above = jnp.minimum(k + 1, levels - 1)

        def load(c, kk):
            ref, base = sources[c]
            return ref[pl.ds(pl.multiple_of((base * levels + kk) * rows, rows), rows), :]

        mid = [load(c, k) for c in range(8)]
        r_lo = [load(c, below) for c in range(8)]
        r_hi = [load(c, above) for c in range(8)]
        left_all = left[...]
        right_all = right[...]
        t_lo, t_hi, p_lo, p_hi = [], [], [], []
        for c in range(8):
            u = mid[c]
            ck = c * levels + k
            t_lo.append(jnp.where(at_up, up[pl.ds(ck, 1), :], pltpu.roll(u, 1, axis=0)))
            t_hi.append(jnp.where(at_down, down[pl.ds(ck, 1), :], pltpu.roll(u, rows - 1, axis=0)))
            p_lo.append(
                jnp.where(at_left, pltpu.roll(left_all, channels - ck, axis=1), pltpu.roll(u, 1, axis=1))
            )
            p_hi.append(
                jnp.where(
                    at_right,
                    pltpu.roll(right_all, channels - 1 - ck, axis=1),
                    pltpu.roll(u, cols - 1, axis=1),
                )
            )

        def dr(c):
            return (r_hi[c] - r_lo[c]) * half_r

        def dth(c):
            return (t_hi[c] - t_lo[c]) * half_t

        def dp(c):
            return (p_hi[c] - p_lo[c]) * half_p

        rr = g_r * g_r
        tt = g_t * g_t
        pp = g_p * g_p

        def laplace(c):
            centre = 2.0 * mid[c]
            return (
                (r_hi[c] + r_lo[c] - centre) * rr
                + (t_hi[c] + t_lo[c] - centre) * tt
                + (p_hi[c] + p_lo[c] - centre) * pp
            )

        v_r, v_t, v_p = mid[1], mid[2], mid[3]
        b_r, b_t, b_p = mid[4], mid[5], mid[6]
        rho, press = mid[0], mid[7]
        div_mom = (
            (r_hi[0] * r_hi[1] - r_lo[0] * r_lo[1]) * half_r
            + (t_hi[0] * t_hi[2] - t_lo[0] * t_lo[2]) * half_t
            + (p_hi[0] * p_hi[3] - p_lo[0] * p_lo[3]) * half_p
        )

        def put(ref, base, x):
            ref[pl.ds(pl.multiple_of((base * levels + k) * rows, rows), rows), :] = x

        put(new_den, 0, rho - dt_step * div_mom)

        grads = [(dr(c), dth(c), dp(c)) for c in range(1, 4)]
        inv_rho = 1.0 / rho
        j_r = dth(6) - dp(5)
        j_t = dp(4) - dr(6)
        j_p = dr(5) - dth(4)
        lorentz = (j_t * b_p - j_p * b_t, j_p * b_r - j_r * b_p, j_r * b_t - j_t * b_r)
        p_grad = (dr(7), dth(7), dp(7))
        for i in range(3):
            g = grads[i]
            carried = v_r * g[0] + v_t * g[1] + v_p * g[2]
            put(
                new_vel, i,
                mid[1 + i]
                + dt_step
                * ((lorentz[i] - p_grad[i]) * inv_rho - carried + diffusivity * laplace(1 + i)),
            )

        def emf(s, i):
            a, b = ((2, 3), (3, 1), (1, 2))[i]
            return s[a] * s[b + 3] - s[b] * s[a + 3]

        def diff(lo, hi, i):
            return emf(hi, i) - emf(lo, i)

        curl = (
            diff(t_lo, t_hi, 2) * half_t - diff(p_lo, p_hi, 1) * half_p,
            diff(p_lo, p_hi, 0) * half_p - diff(r_lo, r_hi, 2) * half_r,
            diff(r_lo, r_hi, 1) * half_r - diff(t_lo, t_hi, 0) * half_t,
        )
        for i in range(3):
            put(new_mag, i, mid[4 + i] + dt_step * (curl[i] + diffusivity * laplace(4 + i)))
        div_flow = grads[0][0] + grads[1][1] + grads[2][2]
        carried = v_r * p_grad[0] + v_t * p_grad[1] + v_p * p_grad[2]
        put(
            new_prs, 0,
            press + dt_step * (diffusivity * laplace(7) - carried - GAMMA * press * div_flow),
        )
        return carry

    lax.fori_loop(0, levels, level, 0)


def body(
    n_theta, n_phi,
    density, velocity, magnetic, pressure, send_row, send_col, send_weight, send_turn, send_dest,
):
    levels, tile_rows, tile_cols = density.shape[1:]
    slots = send_row.shape[-1]
    dims = (n_theta, n_phi, levels, tile_rows, tile_cols, slots)
    channels = 8 * levels
    chunks = -(-slots // LANES)
    total_theta = n_theta * tile_rows
    _, d_phi, _, _ = grid_constants(total_theta, n_phi * tile_cols)
    d_theta = 0.5 * math.pi / total_theta
    fields = [x.reshape(-1, tile_cols) for x in (density, velocity, magnetic, pressure)]
    vmem = pl.BlockSpec(memory_space=pltpu.VMEM)
    f32 = jnp.float32
    dma = pltpu.SemaphoreType.DMA
    tile_row = jax.ShapeDtypeStruct((channels, tile_cols), f32)
    tile_col = jax.ShapeDtypeStruct((tile_rows, channels), f32)
    up, down, left, right = pl.pallas_call(
        functools.partial(exchange_kernel, dims),
        out_shape=(tile_row, tile_row, tile_col, tile_col),
        in_specs=[vmem] * 9,
        out_specs=(vmem,) * 4,
        scratch_shapes=[
            pltpu.VMEM((LANES, chunks * LANES), f32),
            pltpu.VMEM((n_phi, HEAD + slots, channels), f32),
            pltpu.VMEM((2, channels, tile_cols), f32),
            pltpu.VMEM((2, channels, tile_cols), f32),
            pltpu.VMEM((2, tile_rows, channels), f32),
            pltpu.VMEM((2, tile_rows, channels), f32),
            pltpu.VMEM((2, tile_cols, channels), f32),
            pltpu.VMEM((n_theta, tile_cols, channels), f32),
            pltpu.VMEM((total_theta, channels), f32),
            pltpu.VMEM((n_theta, tile_rows, channels), f32),
            dma((n_phi - 1,)),
            dma((n_phi - 1,)),
            dma((2,)),
            dma((n_theta,)),
            dma((n_theta,)),
            dma((n_theta,)),
            dma((4,)),
            dma((4,)),
        ],
        compiler_params=pltpu.CompilerParams(collective_id=0, has_side_effects=True),
        name="exchange",
    )(
        *fields,
        send_row.reshape(1, slots),
        send_col.reshape(1, slots),
        send_weight.reshape(2, slots),
        send_turn.reshape(1, slots),
        send_dest.reshape(1, slots),
    )
    thetas = 0.25 * math.pi + (np.arange(total_theta) + 0.5) * d_theta
    metric = np.broadcast_to(
        (1.0 / (np.sin(thetas) * d_phi))[:, None], (total_theta, tile_cols)
    ).astype(np.float32)
    radius = R_BASE + (np.arange(levels) + 0.5) * DR_STEP
    outs = pl.pallas_call(
        functools.partial(stencil_kernel, dims),
        out_shape=tuple(jax.ShapeDtypeStruct(x.shape, f32) for x in fields),
        in_specs=[vmem] * 9 + [pl.BlockSpec(memory_space=pltpu.SMEM)],
        out_specs=(vmem,) * 4,
        name="stencil",
    )(*fields, up, down, left, right, jnp.asarray(metric), jnp.asarray((1.0 / radius).astype(np.float32)))
    return tuple(
        x.reshape(like.shape) for x, like in zip(outs, (density, velocity, magnetic, pressure))
    )


def solution(mesh):
    scalar = P("patch", None, "theta", "phi")
    vector = P("patch", None, None, "theta", "phi")
    slot = P("patch", "theta", "phi", None)
    return jax.shard_map(
        functools.partial(body, mesh.shape["theta"], mesh.shape["phi"]),
        mesh=mesh,
        in_specs=(
            scalar, vector, vector, scalar, slot, slot,
            P("patch", "theta", "phi", None, None), slot, slot,
        ),
        out_specs=(scalar, vector, vector, scalar),
        check_vma=False,
    )
```

time: 171 us -> 24.5 us (0.14)
  local copies, waits for them, and re-layouts: 68.2 us -> 0 us
  blocking collectives: 45.3 us -> 0 us
  Pallas kernels: 0 us -> 23.7 us
  other arithmetic: 21.8 us -> 0 us
  between operations: 16.9 us -> 0.64 us
  starting transfers between devices: 10 us -> 0 us
  waiting for transfers between devices: 5.58 us -> 0 us
  matrix products: 1.73 us -> 0 us
    scatter x4 -> x0, local copies, waits for them, and re-layouts: 36.7 us -> none  [the longest x1 23.2 us: body(): padded.at[:, 1:-1, 1:-1, -1]]
    psum x1 -> x0, blocking collectives: 28.6 us -> none  [body(): lax.psum(jnp.where(slot_mask, lat_part[None], 0.0), ('patch', 'phi'))]
    pallas_call x0 -> x2, Pallas kernels: none -> 23.7 us  [the longest x1 19 us: body(): pl.pallas_call(functools.partial(exchange_kernel, dims), out_shape=(tile_...]
    ppermute x4 -> x0, starting transfers between devices: 9.94 us -> none  [the longest x2 7.18 us: with_halo(): lax.ppermute(tail, axis, [(i, (i + 1) % count) for i in range(ends)])]
    all_gather x1 -> x0, blocking collectives: 9.12 us -> none  [body(): lon_values = lax.all_gather(donor_rows, 'phi', axis=0, tiled=True)]
    unnamed x40 -> x0, local copies, waits for them, and re-layouts: 8.56 us -> none
    select_n x11 -> x0, other arithmetic: 7.64 us -> none  [the longest x1 2.41 us: body(): jnp.where(phi_index == 0, left_side, padded[:, 1:-1, 1:-1, 0])]
    unnamed x1 -> x0, blocking collectives: 7.56 us -> none
  transfers between devices with their start and end apart: 6 -> 0, of which waited for: 2 -> 0; matrix products, arithmetic and copies ran while one was open for 13% -> 0% of each run, Pallas kernels for 0% -> 0%
where the time goes in v1:
time: 24.5 us; the launch traced here: 24.3 us
  Pallas kernels  23.7 us (97%)
  between operations  0.64 us (3%)
    pallas_call x1, Pallas kernels, body(): pl.pallas_call(functools.partial(exchange_kernel, dims), out_shape=(tile_...  19 us
    pallas_call x1, Pallas kernels, body(): pl.pallas_call(functools.partial(stencil_kernel, dims), out_shape=tuple((...  4.72 us

profile of v1, /device:TPU:0, one launch (start us, length us, event | category | flops | bytes accessed | tf_op | source)
XLA Modules:
  0.0 24.3 jit_solution(16580227964514928462)
XLA Ops:
  0.6 19.0 %exchange.1 = (f32[128,128]{1,0:T(8,128)}, f32[128,128]{1,0:T(8,128)}, f32[16,128]{1,0:T(8,128)}, f32[16,128]{1,0:T(8,128)}) custom-call(f32[256,128]{1,0:T(8,128)} %bitcast.17, f32[768,128]{1,0:T(8,128)} %bitcast.13, f32[768,128]{1,0:T(8,128)} %bitcast.15, f32[256,128]{1,0:T(8,128)} %bitcast.19, s32[1,144]{1,0:T(1,128)} %bitcast.22, s32[1,144]{1,0:T(1,128)} %bitcast.23, ...), custom_call_target="tpu_custom_call" | custom-call | tf_op jit(solution)/shard_map/exchange/pallas_call | solution.py:508
  19.6 4.7 %stencil.1 = (f32[256,128]{1,0:T(8,128)}, f32[768,128]{1,0:T(8,128)}, f32[768,128]{1,0:T(8,128)}, f32[256,128]{1,0:T(8,128)}) custom-call(f32[256,128]{1,0:T(8,128)} %bitcast.18, f32[768,128]{1,0:T(8,128)} %bitcast.14, f32[768,128]{1,0:T(8,128)} %bitcast.16, f32[256,128]{1,0:T(8,128)} %bitcast.20, f32[128,128]{1,0:T(8,128)} %get-tuple-element.12.up, ...), custom_call_target="tpu_custom_call" | custom-call | tf_op jit(solution)/shard_map/stencil/pallas_call | solution.py:548

commit v2 on v1

--- a/solution.py
+++ b/solution.py
@@ -80,71 +80,96 @@
     turn = sturn[...]
     table[4:5, :slots] = jnp.cos(turn)
     table[5:6, :slots] = jnp.sin(turn)
-    dest_row = sdest[...].astype(jnp.float32)
-    table[6:7, :slots] = dest_row
+    table[6:7, :slots] = sdest[...].astype(jnp.float32)
     columns = table[...].T[:slots]
     row_s = columns[:, 0:1]
     col_s = columns[:, 1:2]
     w_row = columns[:, 2:3]
     w_col = columns[:, 3:4]
-    cos_s = columns[:, 4:5]
-    sin_s = columns[:, 5:6]
+    half = slots // 2
+    width = channels // 2
+    fold_lane = lax.broadcasted_iota(jnp.int32, (half, channels), 1)
+    lower = fold_lane < width
+
+    def fold(x):
+        return jnp.where(lower, x[:half], x[half:])
 
     lane = lax.broadcasted_iota(jnp.int32, (slots, tile_cols), 1).astype(jnp.float32)
     pick = jnp.where(lane == col_s, 1.0 - w_col, 0.0) + jnp.where(lane == col_s + 1.0, w_col, 0.0)
     pick_hi, pick_lo = split(pick)
-
-    def field_row(r):
-        return jnp.concatenate(
-            [
+    row_f = fold(row_s)
+    w_row_f = fold(w_row)
+    cos_f = fold(columns[:, 4:5])
+    sin_f = fold(columns[:, 5:6])
+    head = table[0:8, :]
+    head_lane = lax.broadcasted_iota(jnp.int32, (1, LANES), 1)
+    own_dest = (
+        head[6:7, :LANES],
+        pltpu.roll(head, chunks * LANES - half, axis=1)[6:7, :LANES],
+    )
+    for c in range(2):
+        gathered[0, f, c:c + 1, :] = jnp.where(head_lane < half, own_dest[c], -1.0)
+
+    def field_row(h, r):
+        if h == 0:
+            parts = [
                 den[pl.ds(r, levels, stride=tile_rows), :],
                 vel[pl.ds(r, 3 * levels, stride=tile_rows), :],
+            ]
+        else:
+            parts = [
                 mag[pl.ds(r, 3 * levels, stride=tile_rows), :],
                 prs[pl.ds(r, levels, stride=tile_rows), :],
-            ],
-            axis=0,
-        )
-
-    value = jnp.zeros((slots, channels), jnp.float32)
-    for r in range(tile_rows):
-        cells = field_row(r)
-        if r == 0:
-            rows_out[0] = cells
-        if r == tile_rows - 1:
-            rows_out[1] = cells
-        hi, lo = split(cells)
-        part = dot_nt(pick_hi, hi) + (dot_nt(pick_hi, lo) + dot_nt(pick_lo, hi))
-        gain = jnp.where(row_s == r, 1.0 - w_row, 0.0) + jnp.where(row_s + 1.0 == r, w_row, 0.0)
-        value = value + gain * part
-    comp = lax.broadcasted_iota(jnp.int32, (slots, channels), 1) // levels
-    first = (comp == 2) | (comp == 5)
-    second = (comp == 3) | (comp == 6)
-    partner = jnp.where(
-        first,
-        pltpu.roll(value, channels - levels, axis=1),
-        pltpu.roll(value, levels, axis=1),
-    )
-    keep = jnp.where(first | second, cos_s, 1.0)
-    mix = jnp.where(first, sin_s, jnp.where(second, -sin_s, 0.0))
-    own = gathered.at[f]
-    own[HEAD:HEAD + slots, :] = keep * value + mix * partner
-    for c in range(chunks):
-        own[c:c + 1, :] = table[6:7, c * LANES:(c + 1) * LANES]
-
+            ]
+        return jnp.concatenate(parts, axis=0)
+
+    def donors(h):
+        value = jnp.zeros((half, channels), jnp.float32)
+        for r in range(tile_rows):
+            cells = field_row(h, r)
+            if r == 0:
+                rows_out[0, h * width:(h + 1) * width] = cells
+            if r == tile_rows - 1:
+                rows_out[1, h * width:(h + 1) * width] = cells
+            hi, lo = split(jnp.concatenate([cells, cells], axis=0))
+            part = dot_nt(pick_hi, hi) + (dot_nt(pick_hi, lo) + dot_nt(pick_lo, hi))
+            gain = jnp.where(row_f == r, 1.0 - w_row_f, 0.0) + jnp.where(row_f + 1.0 == r, w_row_f, 0.0)
+            value = value + gain * fold(part)
+        comp = lax.rem(fold_lane, width) // levels + 4 * h
+        first = (comp == 2) | (comp == 5)
+        second = (comp == 3) | (comp == 6)
+        partner = jnp.where(
+            first,
+            pltpu.roll(value, channels - levels, axis=1),
+            pltpu.roll(value, levels, axis=1),
+        )
+        keep = jnp.where(first | second, cos_f, 1.0)
+        mix = jnp.where(first, sin_f, jnp.where(second, -sin_f, 0.0))
+        gathered[h, f, HEAD:HEAD + half, :] = keep * value + mix * partner
+
+    def donor_ref(h, source):
+        if h == 0:
+            return gathered.at[0, source]
+        return gathered.at[1, source, pl.ds(HEAD, half)]
+
+    def gather_copy(h, d, source=None):
+        at = f if source is None else source
+        return pltpu.make_async_remote_copy(
+            src_ref=donor_ref(h, at),
+            dst_ref=donor_ref(h, at),
+            send_sem=gather_send.at[h * (n_phi - 1) + d - 1],
+            recv_sem=gather_recv.at[h * (n_phi - 1) + d - 1],
+            device_id=(q, t, lax.rem(f + d, n_phi) if source is None else source),
+            device_id_type=MESH,
+        )
+
+    donors(0)
     pl.semaphore_wait(barrier, n_phi - 1 + 2 + n_theta)
-
-    def gather_copy(d):
-        return pltpu.make_async_remote_copy(
-            src_ref=gathered.at[f],
-            dst_ref=gathered.at[f],
-            send_sem=gather_send.at[d - 1],
-            recv_sem=gather_recv.at[d - 1],
-            device_id=(q, t, lax.rem(f + d, n_phi)),
-            device_id_type=MESH,
-        )
-
     for d in range(1, n_phi):
-        gather_copy(d).start()
+        gather_copy(0, d).start()
+    donors(1)
+    for d in range(1, n_phi):
+        gather_copy(1, d).start()
 
     def row_copy(way):
         return pltpu.make_async_remote_copy(
@@ -196,13 +221,12 @@
         [ids_top, ids_top + total_phi, ids_of(total_theta) + lat_base], axis=0
     ).astype(jnp.float32)
 
-    def place(slot_ref):
+    def place(h, source):
+        folded = gathered[h, source, HEAD:HEAD + half, :]
         total = None
-        for c in range(chunks):
-            size = min(LANES, slots - c * LANES)
-            hits = jnp.where(ids == slot_ref[c:c + 1, :], 1.0, 0.0).astype(jnp.bfloat16)
-            hi, lo = split(slot_ref[HEAD + c * LANES:HEAD + c * LANES + size, :])
-            hits = hits[:, :size]
+        for c in range(2):
+            hits = jnp.where(ids == gathered[0, source, c:c + 1, :], 1.0, 0.0).astype(jnp.bfloat16)[:, :half]
+            hi, lo = split(folded if c == 0 else pltpu.roll(folded, width, axis=1))
             term = dot_nn(hits, hi) + dot_nn(hits, lo)
             total = term if total is None else total + term
         return total
@@ -215,31 +239,38 @@
     def _():
         col_copy(1).start()
 
-    placed = place(gathered.at[f])
-    for d in range(1, n_phi):
-        source = lax.rem(f + n_phi - d, n_phi)
-        pltpu.make_async_remote_copy(
-            src_ref=gathered.at[source],
-            dst_ref=gathered.at[source],
-            send_sem=gather_send.at[d - 1],
-            recv_sem=gather_recv.at[d - 1],
-            device_id=(q, t, source),
-            device_id_type=MESH,
-        ).wait_recv()
-        placed = placed + place(gathered.at[source])
-    lon_out[0] = placed[:tile_cols]
-    lon_out[1] = placed[tile_cols:2 * tile_cols]
-    lat_out[...] = placed[2 * tile_cols:]
-
-    def lon_copy(side):
+    short = tile_cols // 2
+    lon_lower = lax.broadcasted_iota(jnp.int32, (short, channels), 1) < width
+
+    def lon_copy(h, side):
         return pltpu.make_async_remote_copy(
-            src_ref=lon_out.at[side],
-            dst_ref=lon_in.at[t],
-            send_sem=lon_send.at[side],
-            recv_sem=lon_recv.at[t],
+            src_ref=lon_out.at[h, side],
+            dst_ref=lon_in.at[h, t],
+            send_sem=lon_send.at[2 * h + side],
+            recv_sem=lon_recv.at[h * n_theta + t],
             device_id=(other, (n_theta - 1) * side, f),
             device_id_type=MESH,
         )
+
+    lat_parts = []
+    for h in range(2):
+        placed = place(h, f)
+        for d in range(1, n_phi):
+            source = lax.rem(f + n_phi - d, n_phi)
+            gather_copy(h, d, source).wait_recv()
+            placed = placed + place(h, source)
+        for side in range(2):
+            base = side * tile_cols
+            lon_out[h, side] = jnp.where(
+                lon_lower,
+                placed[base:base + short],
+                pltpu.roll(placed[base + short:base + tile_cols], width, axis=1),
+            )
+        lat_parts.append(placed[2 * tile_cols:])
+        lon_copy(h, 0).start()
+        lon_copy(h, 1).start()
+    lat_lower = lax.broadcasted_iota(jnp.int32, (total_theta, channels), 1) < width
+    lat_out[...] = jnp.where(lat_lower, lat_parts[0], pltpu.roll(lat_parts[1], width, axis=1))
 
     def lat_copy(d):
         return pltpu.make_async_remote_copy(
@@ -251,9 +282,6 @@
             device_id_type=MESH,
         )
 
-    lon_copy(0).start()
-    lon_copy(1).start()
-
     at_side = (f == 0) | (f == n_phi - 1)
     at_end = (t == 0) | (t == n_theta - 1)
 
@@ -284,18 +312,27 @@
 
     @pl.when(at_end)
     def _():
-        for s in range(n_theta):
-            pltpu.make_async_remote_copy(
-                src_ref=lon_in.at[s],
-                dst_ref=lon_in.at[s],
-                send_sem=lon_send.at[0],
-                recv_sem=lon_recv.at[s],
-                device_id=(other, s, f),
-                device_id_type=MESH,
-            ).wait_recv()
-        total = lon_in[0]
-        for s in range(1, n_theta):
-            total = total + lon_in[s]
+        sums = []
+        for h in range(2):
+            total = None
+            for s in range(n_theta):
+                pltpu.make_async_remote_copy(
+                    src_ref=lon_in.at[h, s],
+                    dst_ref=lon_in.at[h, s],
+                    send_sem=lon_send.at[0],
+                    recv_sem=lon_recv.at[h * n_theta + s],
+                    device_id=(other, s, f),
+                    device_id_type=MESH,
+                ).wait_recv()
+                total = lon_in[h, s] if total is None else total + lon_in[h, s]
+            sums.append(total)
+        total = jnp.concatenate(
+            [
+                jnp.where(lon_lower, sums[0], pltpu.roll(sums[1], width, axis=1)),
+                jnp.where(lon_lower, pltpu.roll(sums[0], width, axis=1), sums[1]),
+            ],
+            axis=0,
+        )
         total = total.T
 
         @pl.when(t == 0)
@@ -329,10 +366,11 @@
         def _():
             right_out[...] = total
 
-    for d in range(1, n_phi):
-        gather_copy(d).wait_send()
-    lon_copy(0).wait_send()
-    lon_copy(1).wait_send()
+    for h in range(2):
+        for d in range(1, n_phi):
+            gather_copy(h, d).wait_send()
+        lon_copy(h, 0).wait_send()
+        lon_copy(h, 1).wait_send()
 
     @pl.when(at_side)
     def _():
@@ -512,25 +550,25 @@
         out_specs=(vmem,) * 4,
         scratch_shapes=[
             pltpu.VMEM((LANES, chunks * LANES), f32),
-            pltpu.VMEM((n_phi, HEAD + slots, channels), f32),
+            pltpu.VMEM((2, n_phi, HEAD + slots // 2, channels), f32),
             pltpu.VMEM((2, channels, tile_cols), f32),
             pltpu.VMEM((2, channels, tile_cols), f32),
             pltpu.VMEM((2, tile_rows, channels), f32),
             pltpu.VMEM((2, tile_rows, channels), f32),
-            pltpu.VMEM((2, tile_cols, channels), f32),
-            pltpu.VMEM((n_theta, tile_cols, channels), f32),
+            pltpu.VMEM((2, 2, tile_cols // 2, channels), f32),
+            pltpu.VMEM((2, n_theta, tile_cols // 2, channels), f32),
             pltpu.VMEM((total_theta, channels), f32),
             pltpu.VMEM((n_theta, tile_rows, channels), f32),
-            dma((n_phi - 1,)),
-            dma((n_phi - 1,)),
-            dma((2,)),
-            dma((n_theta,)),
+            dma((2 * (n_phi - 1),)),
+            dma((2 * (n_phi - 1),)),
+            dma((4,)),
+            dma((2 * n_theta,)),
             dma((n_theta,)),
             dma((n_theta,)),
             dma((4,)),
             dma((4,)),
         ],
-        compiler_params=pltpu.CompilerParams(collective_id=0, has_side_effects=True),
+        compiler_params=pltpu.CompilerParams(collective_id=0, has_side_effects=True, vmem_limit_bytes=16 << 20),
         name="exchange",
     )(
         *fields,
@@ -550,7 +588,7 @@
         out_shape=tuple(jax.ShapeDtypeStruct(x.shape, f32) for x in fields),
         in_specs=[vmem] * 9 + [pl.BlockSpec(memory_space=pltpu.SMEM)],
         out_specs=(vmem,) * 4,
-        name="stencil",
+        compiler_params=pltpu.CompilerParams(vmem_limit_bytes=16 << 20), name="stencil",
     )(*fields, up, down, left, right, jnp.asarray(metric), jnp.asarray((1.0 / radius).astype(np.float32)))
     return tuple(
         x.reshape(like.shape) for x, like in zip(outs, (density, velocity, magnetic, pressure))

time: 24.5 us -> 26.4 us (1.078)
  local copies, waits for them, and re-layouts: 0 us -> 5.14 us
  Pallas kernels: 23.7 us -> 20.3 us
    unnamed x0 -> x22, local copies, waits for them, and re-layouts: none -> 5.14 us
    pallas_call x1, Pallas kernels: 19 us -> 16.3 us  [body(): pl.pallas_call(functools.partial(exchange_kernel, dims), out_shape=(tile_...]
    pallas_call x1, Pallas kernels: 4.72 us -> 4 us  [body(): pl.pallas_call(functools.partial(stencil_kernel, dims), out_shape=tuple((...]
where the time goes in v2:
time: 26.4 us; the launch traced here: 26.1 us
  Pallas kernels  20.3 us (77%)
  local copies, waits for them, and re-layouts  5.14 us (19%)
  between operations  0.71 us (3%)
    pallas_call x1, Pallas kernels, body(): pl.pallas_call(functools.partial(exchange_kernel, dims), out_shape=(tile_...  16.3 us
    unnamed x22, local copies, waits for them, and re-layouts  5.14 us
    pallas_call x1, Pallas kernels, body(): pl.pallas_call(functools.partial(stencil_kernel, dims), out_shape=tuple((...  4 us

profile of v2, /device:TPU:0, one launch (start us, length us, event | category | flops | bytes accessed | tf_op | source)
XLA Modules:
  0.0 26.1 jit_solution(18386974191724645207)
XLA Ops:
  0.6 0.0 copy-start.9
  0.6 0.0 copy-start.7
  0.7 0.0 copy-start.8
  0.7 0.0 copy-start.5
  0.7 0.0 copy-start.6
  0.7 0.6 %copy-done.9 = s32[1,1,1,144]{3,2,1,0:T(1,128)S(1)} copy-done((s32[1,1,1,144]{3,2,1,0:T(1,128)S(1)}, s32[1,1,1,144]{3,2,1,0:T(1,128)}, u32[]{:S(2)}) %copy-start.9) | copy-done | bytes 600
  1.3 0.0 copy-done.7
  1.3 0.0 copy-done.8
  1.3 0.0 copy-done.5
  1.4 0.0 copy-done.6
  1.4 0.0 copy-start
  1.4 1.0 %copy-done = f32[1,3,16,16,128]{4,3,2,1,0:T(8,128)S(1)} copy-done((f32[1,3,16,16,128]{4,3,2,1,0:T(8,128)S(1)}, f32[1,3,16,16,128]{4,3,2,1,0:T(8,128)}, u32[]{:S(2)}) %copy-start) | copy-done | bytes 393240
  2.4 0.0 copy-start.1
  2.4 1.0 %copy-done.1 = f32[1,3,16,16,128]{4,3,2,1,0:T(8,128)S(1)} copy-done((f32[1,3,16,16,128]{4,3,2,1,0:T(8,128)S(1)}, f32[1,3,16,16,128]{4,3,2,1,0:T(8,128)}, u32[]{:S(2)}) %copy-start.1) | copy-done | bytes 393240
  3.4 0.0 copy-start.2
  3.4 0.9 %copy-done.2 = f32[1,16,16,128]{3,2,1,0:T(8,128)S(1)} copy-done((f32[1,16,16,128]{3,2,1,0:T(8,128)S(1)}, f32[1,16,16,128]{3,2,1,0:T(8,128)}, u32[]{:S(2)}) %copy-start.2) | copy-done | bytes 131096
  4.3 0.0 copy-start.3
  4.3 0.9 %copy-done.3 = f32[1,16,16,128]{3,2,1,0:T(8,128)S(1)} copy-done((f32[1,16,16,128]{3,2,1,0:T(8,128)S(1)}, f32[1,16,16,128]{3,2,1,0:T(8,128)}, u32[]{:S(2)}) %copy-start.3) | copy-done | bytes 131096
  5.2 0.0 copy-start.4
  5.2 16.3 %exchange.1 = (f32[128,128]{1,0:T(8,128)S(1)}, f32[128,128]{1,0:T(8,128)S(1)}, f32[16,128]{1,0:T(8,128)S(1)}, f32[16,128]{1,0:T(8,128)S(1)}) custom-call(f32[256,128]{1,0:T(8,128)S(1)} %bitcast.17, f32[768,128]{1,0:T(8,128)S(1)} %bitcast.13, f32[768,128]{1,0:T(8,128)S(1)} %bitcast.15, f32[256,128]{1,0:T(8,128)S(1)} %bitcast.19, s32[1,144]{1,0:T(1,128)S(1)} %bitcast.22, ...), custom_call_target="tpu_custom_call" | custom-call | tf_op jit(solution)/shard_map/exchange/pallas_call | solution.py:546
  21.5 0.0 copy-start.10
  21.5 0.0 copy-done.4
  21.5 0.6 %copy-done.10 = f32[16]{0:T(128)S(1)} copy-done((f32[16]{0:T(128)S(1)}, f32[16]{0:T(128)}, u32[]{:S(2)}) %copy-start.10) | copy-done | bytes 88
  22.1 4.0 %stencil.1 = (f32[256,128]{1,0:T(8,128)}, f32[768,128]{1,0:T(8,128)}, f32[768,128]{1,0:T(8,128)}, f32[256,128]{1,0:T(8,128)}) custom-call(f32[256,128]{1,0:T(8,128)S(1)} %bitcast.18, f32[768,128]{1,0:T(8,128)S(1)} %bitcast.14, f32[768,128]{1,0:T(8,128)S(1)} %bitcast.16, f32[256,128]{1,0:T(8,128)S(1)} %bitcast.20, f32[128,128]{1,0:T(8,128)S(1)} %get-tuple-element.12.up, ...), custom_call_target="tpu_custom_call" | custom-call | tf_op jit(solution)/shard_map/stencil/pallas_call | solution.py:586
Async XLA Ops:
  0.6 0.7 %copy-start.9 = (s32[1,1,1,144]{3,2,1,0:T(1,128)S(1)}, s32[1,1,1,144]{3,2,1,0:T(1,128)}, u32[]{:S(2)}) copy-start(s32[1,1,1,144]{3,2,1,0:T(1,128)} %param.19) | copy-start | bytes 1732
  0.6 0.7 %copy-start.7 = (s32[1,1,1,144]{3,2,1,0:T(1,128)S(1)}, s32[1,1,1,144]{3,2,1,0:T(1,128)}, u32[]{:S(2)}) copy-start(s32[1,1,1,144]{3,2,1,0:T(1,128)} %param.16) | copy-start | bytes 1732
  0.7 0.7 %copy-start.8 = (f32[1,1,1,144]{3,2,1,0:T(1,128)S(1)}, f32[1,1,1,144]{3,2,1,0:T(1,128)}, u32[]{:S(2)}) copy-start(f32[1,1,1,144]{3,2,1,0:T(1,128)} %param.18) | copy-start | bytes 1732
  0.7 0.7 %copy-start.5 = (f32[1,1,1,2,144]{4,3,2,1,0:T(2,128)S(1)}, f32[1,1,1,2,144]{4,3,2,1,0:T(2,128)}, u32[]{:S(2)}) copy-start(f32[1,1,1,2,144]{4,3,2,1,0:T(2,128)} %param.17) | copy-start | bytes 3460
  0.7 0.7 %copy-start.6 = (s32[1,1,1,144]{3,2,1,0:T(1,128)S(1)}, s32[1,1,1,144]{3,2,1,0:T(1,128)}, u32[]{:S(2)}) copy-start(s32[1,1,1,144]{3,2,1,0:T(1,128)} %param.15) | copy-start | bytes 1732
  1.4 1.0 %copy-start = (f32[1,3,16,16,128]{4,3,2,1,0:T(8,128)S(1)}, f32[1,3,16,16,128]{4,3,2,1,0:T(8,128)}, u32[]{:S(2)}) copy-start(f32[1,3,16,16,128]{4,3,2,1,0:T(8,128)} %param.12) | copy-start | bytes 1179652
  2.4 1.0 %copy-start.1 = (f32[1,3,16,16,128]{4,3,2,1,0:T(8,128)S(1)}, f32[1,3,16,16,128]{4,3,2,1,0:T(8,128)}, u32[]{:S(2)}) copy-start(f32[1,3,16,16,128]{4,3,2,1,0:T(8,128)} %param.13) | copy-start | bytes 1179652
  3.4 0.9 %copy-start.2 = (f32[1,16,16,128]{3,2,1,0:T(8,128)S(1)}, f32[1,16,16,128]{3,2,1,0:T(8,128)}, u32[]{:S(2)}) copy-start(f32[1,16,16,128]{3,2,1,0:T(8,128)} %param.11) | copy-start | bytes 393220
  4.3 0.9 %copy-start.3 = (f32[1,16,16,128]{3,2,1,0:T(8,128)S(1)}, f32[1,16,16,128]{3,2,1,0:T(8,128)}, u32[]{:S(2)}) copy-start(f32[1,16,16,128]{3,2,1,0:T(8,128)} %param.14) | copy-start | bytes 393220
  5.2 16.3 %copy-start.4 = (f32[64,128]{1,0:T(8,128)S(1)}, f32[64,128]{1,0:T(8,128)}, u32[]{:S(2)}) copy-start(f32[64,128]{1,0:T(8,128)} %constant.4.clone.metric) | copy-start | bytes 98308
  21.5 0.7 %copy-start.10 = (f32[16]{0:T(128)S(1)}, f32[16]{0:T(128)}, u32[]{:S(2)}) copy-start(f32[16]{0:T(128)} %constant.5.clone.inv_radius) | copy-start | bytes 196

commit v3 on v2

--- a/solution.py
+++ b/solution.py
@@ -46,8 +46,9 @@
 
 
 def exchange_kernel(
-    dims, den, vel, mag, prs, srow, scol, swgt, sturn, sdest,
+    dims, den_hbm, vel_hbm, mag_hbm, prs_hbm, srow_hbm, scol_hbm, swgt_hbm, sturn_hbm, sdest_hbm,
     up_out, down_out, left_out, right_out,
+    den, vel, mag, prs, srow, scol, swgt, sturn, sdest, load_sem,
     table, gathered, rows_out, rows_in, cols_out, cols_in, lon_out, lon_in, lat_out, lat_in,
     gather_send, gather_recv, lon_send, lon_recv, lat_send, lat_recv, halo_send, halo_recv,
 ):
@@ -61,6 +62,14 @@
     f = lax.axis_index("phi")
     other = 1 - q
 
+    pairs = (
+        (srow_hbm, srow), (scol_hbm, scol), (swgt_hbm, swgt), (sturn_hbm, sturn), (sdest_hbm, sdest),
+        (den_hbm, den), (vel_hbm, vel), (mag_hbm, mag), (prs_hbm, prs),
+    )
+    loads = [pltpu.make_async_copy(a, b, load_sem.at[i]) for i, (a, b) in enumerate(pairs)]
+    for load in loads:
+        load.start()
+
     barrier = pltpu.get_barrier_semaphore()
 
     def greet(device):
@@ -74,6 +83,8 @@
         greet((other, d, f))
 
     table[...] = jnp.zeros_like(table)
+    for load in loads[:5]:
+        load.wait()
     table[0:1, :slots] = srow[...].astype(jnp.float32)
     table[1:2, :slots] = scol[...].astype(jnp.float32)
     table[2:4, :slots] = swgt[...]
@@ -163,10 +174,14 @@
             device_id_type=MESH,
         )
 
+    loads[5].wait()
+    loads[6].wait()
     donors(0)
     pl.semaphore_wait(barrier, n_phi - 1 + 2 + n_theta)
     for d in range(1, n_phi):
         gather_copy(0, d).start()
+    loads[7].wait()
+    loads[8].wait()
     donors(1)
     for d in range(1, n_phi):
         gather_copy(1, d).start()
@@ -395,14 +410,49 @@
 
 
 def stencil_kernel(
-    dims, den, vel, mag, prs, up, down, left, right, metric, inv_radius,
-    new_den, new_vel, new_mag, new_prs,
+    dims, parts, den_hbm, vel_hbm, mag_hbm, prs_hbm, up_hbm, down_hbm, left_hbm, right_hbm, metric_hbm,
+    inv_radius, den_out, vel_out, mag_out, prs_out,
+    den, vel, mag, prs, up, down, left, right, metric, new_den, new_vel, new_mag, new_prs,
+    ghost_sem, load_sem, store_sem,
 ):
     n_theta, n_phi, levels, rows, cols, _ = dims
     d_theta, _, dt_step, diffusivity = grid_constants(rows * n_theta, cols * n_phi)
     g_r = 1.0 / DR_STEP
+    span = levels // parts
     first_row = pl.multiple_of(lax.axis_index("theta") * rows, rows)
-    lon_row = metric[pl.ds(first_row, rows), :]
+    ghosts = [
+        pltpu.make_async_copy(a, b, ghost_sem.at[i])
+        for i, (a, b) in enumerate(
+            (
+                (up_hbm, up), (down_hbm, down), (left_hbm, left), (right_hbm, right),
+                (metric_hbm.at[pl.ds(first_row, rows)], metric),
+            )
+        )
+    ]
+
+    def pieces(sources, targets, sems, part):
+        rows_of = pl.ds(part * span * rows, span * rows)
+        return [
+            pltpu.make_async_copy(a.at[:, rows_of], b.at[:, rows_of], sems.at[part, i])
+            for i, (a, b) in enumerate(zip(sources, targets))
+        ]
+
+    loads = [
+        pieces((den_hbm, vel_hbm, mag_hbm, prs_hbm), (den, vel, mag, prs), load_sem, part)
+        for part in range(parts)
+    ]
+    stores = [
+        pieces((new_den, new_vel, new_mag, new_prs), (den_out, vel_out, mag_out, prs_out), store_sem, part)
+        for part in range(parts)
+    ]
+    for copy in loads[0] + ghosts:
+        copy.start()
+    for part in range(1, parts):
+        for copy in loads[part]:
+            copy.start()
+    for copy in ghosts + loads[0]:
+        copy.wait()
+    lon_row = metric[...]
     row_id = lax.broadcasted_iota(jnp.int32, (rows, cols), 0)
     col_id = lax.broadcasted_iota(jnp.int32, (rows, cols), 1)
     at_up = row_id == 0
@@ -424,7 +474,7 @@
 
         def load(c, kk):
             ref, base = sources[c]
-            return ref[pl.ds(pl.multiple_of((base * levels + kk) * rows, rows), rows), :]
+            return ref[base, pl.ds(pl.multiple_of(kk * rows, rows), rows), :]
 
         mid = [load(c, k) for c in range(8)]
         r_lo = [load(c, below) for c in range(8)]
@@ -479,7 +529,7 @@
         )
 
         def put(ref, base, x):
-            ref[pl.ds(pl.multiple_of((base * levels + k) * rows, rows), rows), :] = x
+            ref[base, pl.ds(pl.multiple_of(k * rows, rows), rows), :] = x
 
         put(new_den, 0, rho - dt_step * div_mom)
 
@@ -522,7 +572,16 @@
         )
         return carry
 
-    lax.fori_loop(0, levels, level, 0)
+    for part in range(parts):
+        if part + 1 < parts:
+            for copy in loads[part + 1]:
+                copy.wait()
+        lax.fori_loop(part * span, (part + 1) * span, level, 0)
+        for copy in stores[part]:
+            copy.start()
+    for part in range(parts):
+        for copy in stores[part]:
+            copy.wait()
 
 
 def body(
@@ -546,9 +605,16 @@
     up, down, left, right = pl.pallas_call(
         functools.partial(exchange_kernel, dims),
         out_shape=(tile_row, tile_row, tile_col, tile_col),
-        in_specs=[vmem] * 9,
+        in_specs=[pl.BlockSpec(memory_space=pl.ANY)] * 9,
         out_specs=(vmem,) * 4,
         scratch_shapes=[
+            *(pltpu.VMEM(x.shape, f32) for x in fields),
+            pltpu.VMEM((1, slots), jnp.int32),
+            pltpu.VMEM((1, slots), jnp.int32),
+            pltpu.VMEM((2, slots), f32),
+            pltpu.VMEM((1, slots), f32),
+            pltpu.VMEM((1, slots), jnp.int32),
+            dma((9,)),
             pltpu.VMEM((LANES, chunks * LANES), f32),
             pltpu.VMEM((2, n_phi, HEAD + slots // 2, channels), f32),
             pltpu.VMEM((2, channels, tile_cols), f32),
@@ -568,7 +634,7 @@
             dma((4,)),
             dma((4,)),
         ],
-        compiler_params=pltpu.CompilerParams(collective_id=0, has_side_effects=True, vmem_limit_bytes=16 << 20),
+        compiler_params=pltpu.CompilerParams(collective_id=0, has_side_effects=True),
         name="exchange",
     )(
         *fields,
@@ -583,13 +649,28 @@
         (1.0 / (np.sin(thetas) * d_phi))[:, None], (total_theta, tile_cols)
     ).astype(np.float32)
     radius = R_BASE + (np.arange(levels) + 0.5) * DR_STEP
+    stacked = [x.reshape(-1, levels * tile_rows, tile_cols) for x in (density, velocity, magnetic, pressure)]
+    parts = 4 if levels % 4 == 0 else 1
+    hbm = pl.BlockSpec(memory_space=pl.ANY)
     outs = pl.pallas_call(
-        functools.partial(stencil_kernel, dims),
-        out_shape=tuple(jax.ShapeDtypeStruct(x.shape, f32) for x in fields),
-        in_specs=[vmem] * 9 + [pl.BlockSpec(memory_space=pltpu.SMEM)],
-        out_specs=(vmem,) * 4,
-        compiler_params=pltpu.CompilerParams(vmem_limit_bytes=16 << 20), name="stencil",
-    )(*fields, up, down, left, right, jnp.asarray(metric), jnp.asarray((1.0 / radius).astype(np.float32)))
+        functools.partial(stencil_kernel, dims, parts),
+        out_shape=tuple(jax.ShapeDtypeStruct(x.shape, f32) for x in stacked),
+        in_specs=[hbm] * 9 + [pl.BlockSpec(memory_space=pltpu.SMEM)],
+        out_specs=(hbm,) * 4,
+        scratch_shapes=[
+            *(pltpu.VMEM(x.shape, f32) for x in stacked),
+            pltpu.VMEM((channels, tile_cols), f32),
+            pltpu.VMEM((channels, tile_cols), f32),
+            pltpu.VMEM((tile_rows, channels), f32),
+            pltpu.VMEM((tile_rows, channels), f32),
+            pltpu.VMEM((tile_rows, tile_cols), f32),
+            *(pltpu.VMEM(x.shape, f32) for x in stacked),
+            dma((5,)),
+            dma((parts, 4)),
+            dma((parts, 4)),
+        ],
+        name="stencil",
+    )(*stacked, up, down, left, right, jnp.asarray(metric), jnp.asarray((1.0 / radius).astype(np.float32)))
     return tuple(
         x.reshape(like.shape) for x, like in zip(outs, (density, velocity, magnetic, pressure))
     )

time: 26.4 us -> 23.6 us (0.89)
  local copies, waits for them, and re-layouts: 5.14 us -> 0 us
  Pallas kernels: 20.3 us -> 22.8 us
    unnamed x22 -> x0, local copies, waits for them, and re-layouts: 5.14 us -> none
    pallas_call x1, Pallas kernels: 4 us -> 5.38 us  [body(): pl.pallas_call(functools.partial(stencil_kernel, dims, parts), out_shape=...]
    pallas_call x1, Pallas kernels: 16.3 us -> 17.4 us  [body(): pl.pallas_call(functools.partial(exchange_kernel, dims), out_shape=(tile_...]
where the time goes in v3:
time: 23.6 us; the launch traced here: 23.4 us
  Pallas kernels  22.8 us (97%)
  between operations  0.64 us (3%)
    pallas_call x1, Pallas kernels, body(): pl.pallas_call(functools.partial(exchange_kernel, dims), out_shape=(tile_...  17.4 us
    pallas_call x1, Pallas kernels, body(): pl.pallas_call(functools.partial(stencil_kernel, dims, parts), out_shape=...  5.38 us

profile of v3, /device:TPU:0, one launch (start us, length us, event | category | flops | bytes accessed | tf_op | source)
XLA Modules:
  0.0 23.4 jit_solution(4863838746045200346)
XLA Ops:
  0.6 17.4 %exchange.1 = (f32[128,128]{1,0:T(8,128)}, f32[128,128]{1,0:T(8,128)}, f32[16,128]{1,0:T(8,128)}, f32[16,128]{1,0:T(8,128)}) custom-call(f32[256,128]{1,0:T(8,128)} %bitcast.21, f32[768,128]{1,0:T(8,128)} %bitcast.17, f32[768,128]{1,0:T(8,128)} %bitcast.19, f32[256,128]{1,0:T(8,128)} %bitcast.23, s32[1,144]{1,0:T(1,128)} %bitcast.26, s32[1,144]{1,0:T(1,128)} %bitcast.27, ...), custom_call_target="tpu_custom_call" | custom-call | tf_op jit(solution)/shard_map/exchange/pallas_call | solution.py:605
  18.1 5.4 %stencil.1 = (f32[1,256,128]{2,1,0:T(8,128)}, f32[3,256,128]{2,1,0:T(8,128)}, f32[3,256,128]{2,1,0:T(8,128)}, f32[1,256,128]{2,1,0:T(8,128)}) custom-call(f32[1,256,128]{2,1,0:T(8,128)} %bitcast.22, f32[3,256,128]{2,1,0:T(8,128)} %bitcast.18, f32[3,256,128]{2,1,0:T(8,128)} %bitcast.20, f32[1,256,128]{2,1,0:T(8,128)} %bitcast.24, ...), custom_call_target="tpu_custom_call" | custom-call | tf_op jit(solution)/shard_map/stencil/pallas_call | solution.py:655
